TPU v7x, 32 devices: a whole 2x2x4 slice. The times are simulated.
32 devices in a mesh: dp: 4 (over y, core), vocab: 8 (over z, x).
Axes of the slice: x: 2, y: 2, z: 4, core: 2. Of those that a mesh axis runs over, the one named last changes fastest.
Arguments:
- hidden: bfloat16 [256, 3584], P('dp'), may hold values from -48 to 48
- embedding: bfloat16 [24576, 3584], P(('dp', 'vocab')), may hold values from -1 to 1
- targets: int32 [256], P('dp'), may hold values from 0 to 24575
- loss_weight: bfloat16 [256], P('dp'), may hold values from 1 to 10
Outputs:
- hidden_grad: bfloat16 [256, 3584], P('dp')
- table_grad: bfloat16 [24576, 3584], P(('dp', 'vocab'))
All inputs are finite; a program needn't handle non-finite values.
Results may differ from a plain program's by a relative error of at most 0.0049.
Values may be sent and summed in bfloat16 or wider, within the bound.
A program may use at most 128 MiB of HBM per device.

v0:
```python
import jax
import jax.numpy as jnp
from jax import lax
from jax.sharding import PartitionSpec as P

soft_cap = 30.0
z_weight = 0.002


def body(hidden, embedding, targets, loss_weight):
    shard_rows = embedding.shape[0]
    group_hidden, group_weight = (
        lax.all_gather(hidden, "dp", axis=0, tiled=True),
        lax.all_gather(loss_weight, "dp", axis=0, tiled=True),
    )
    group_targets = lax.all_gather(targets, "dp", axis=0, tiled=True)
    logits = lax.dot_general(
        group_hidden, embedding, (((1,), (1,)), ((), ())), preferred_element_type=jnp.float32
    )
    capped = soft_cap * jnp.tanh(logits / soft_cap)
    exp_terms = jnp.exp(capped - soft_cap)
    partial_value = jnp.sum(exp_terms, axis=1)
    weight = group_weight.astype(jnp.float32)
    device_place = lax.axis_index("dp") * lax.axis_size("vocab") + lax.axis_index("vocab")
    exp_total = lax.psum(partial_value, ("dp", "vocab"))
    factor = weight * (1.0 + 2.0 * z_weight * (soft_cap + jnp.log(exp_total))) / exp_total
    columns = device_place * shard_rows + lax.iota(jnp.int32, shard_rows)
    target_hit = group_targets[:, None] == columns[None, :]
    softmax_part = factor[:, None] * exp_terms - jnp.where(target_hit, weight[:, None], 0.0)
    scores_grad = (softmax_part * (1.0 - (capped / soft_cap) ** 2)).astype(jnp.bfloat16)
    table_grad = lax.dot_general(
        scores_grad, group_hidden, (((0,), (0,)), ((), ())), preferred_element_type=jnp.float32
    ).astype(jnp.bfloat16)
    group_grad = lax.psum_scatter(
        jnp.dot(scores_grad, embedding, preferred_element_type=jnp.float32),
        "dp",
        scatter_dimension=0,
        tiled=True,
    )
    hidden_grad = lax.psum(group_grad, "vocab").astype(jnp.bfloat16)
    return (hidden_grad, table_grad)


def solution(mesh):
    return jax.shard_map(
        body,
        mesh=mesh,
        in_specs=(P("dp", None), P(("dp", "vocab"), None), P("dp"), P("dp")),
        out_specs=(P("dp", None), P(("dp", "vocab"), None)),
        check_vma=False,
    )
```

profile of v0, /device:TPU:0, one launch (start us, length us, event | category | flops | bytes accessed | tf_op | source)
XLA Modules:
  0.0 182.5 jit_solution(10813239611045289594)
XLA Ops:
  7.2 0.0 all-gather.2.cloned.1.call-start
  7.2 0.7 all-gather.2.cloned.1.call-update
  7.9 0.0 reduce-scatter.2.cloned.1.call-start
  8.0 1.2 dynamic-slice
  9.9 0.9 dynamic-update-slice
  10.7 8.4 %all-reduce = bf16[256]{0:T(256)(128)(2,1)S(1)} all-reduce(bf16[256]{0:T(256)(128)(2,1)S(1)} %dynamic-update-slice), channel_id=1, replica_groups=mesh['dp'=4,'vocab'=8] {'dp'}, use_global_device_ids=true, to_apply=%add | all-reduce | flops 256 | bytes 1024
  19.1 0.9 dynamic-update-slice.1
  20.0 4.5 %all-reduce.1 = s32[256]{0:T(256)S(1)} all-reduce(s32[256]{0:T(256)S(1)} %dynamic-update-slice.1), channel_id=1, replica_groups=mesh['dp'=4,'vocab'=8] {'dp'}, use_global_device_ids=true, to_apply=%add.1 | all-reduce | flops 256 | bytes 2048
  24.4 9.0 %all-gather.2.cloned.1.call-done = bf16[256,3584]{1,0:T(8,128)(2,1)} async-done(((bf16[64,3584]{1,0:T(8,128)(2,1)}), bf16[256,3584]{1,0:T(8,128)(2,1)}) %all-gather.2.cloned.1.call-update) | async-done | bytes 1835024 | tf_op jit(solution)/shard_map/all_gather | solution.py:13
  33.5 4.9 %fusion.1 = (f32[256]{0:T(256)S(1)}, f32[256,768]{1,0:T(8,128)S(1)}) fusion(bf16[256,3584]{1,0:T(8,128)(2,1)} %all-gather.2.cloned.1.call-done, bf16[768,3584]{1,0:T(8,128)(2,1)} %param.5), kind=kOutput, calls=%fused_computation.5 | convolution fusion | flops 1410072320 | bytes 8127488 | tf_op jit(solution)/shard_map/dot_general | solution.py:17
  38.4 39.3 %psum.14 = f32[256]{0:T(256)S(1)} all-reduce(f32[256]{0:T(256)S(1)} %get-tuple-element.2), channel_id=1, replica_groups=mesh['dp'=4,'vocab'=8] {'dp','vocab'}, use_global_device_ids=true, to_apply=%region_1.0 | all-reduce | flops 256 | bytes 2048 | tf_op jit(solution)/shard_map/psum | solution.py:25
  77.7 0.0 copy-start
  77.7 6.3 %fusion.2 = f32[256,3584]{1,0:T(8,128)} fusion(bf16[768,3584]{1,0:T(8,128)(2,1)} %param.5, f32[256,768]{1,0:T(8,128)S(1)} %get-tuple-element.3, f32[256]{0:T(256)S(1)} %convert_element_type.12, s32[768]{0:T(1024)S(1)} %iota_add_fusion, f32[256]{0:T(256)S(1)} %multiply_divide_fusion, s32[256]{0:T(256)S(1)} %all-reduce.1), kind=kOutput, calls=%fused_computation.8 | convolution fusion | flops 1411252224 | bytes 9967616 | tf_op jit(solution)/shard_map/dot_general | solution.py:35
  84.0 0.0 reduce-scatter.2.cloned.1.call-update
  84.0 0.0 copy-done
  84.0 4.3 %convolution_convert_fusion = bf16[768,3584]{1,0:T(8,128)(2,1)} fusion(bf16[256,3584]{1,0:T(8,128)(2,1)S(1)} %copy-done, f32[256,768]{1,0:T(8,128)S(1)} %get-tuple-element.3, f32[256]{0:T(256)S(1)} %convert_element_type.12, s32[768]{0:T(1024)S(1)} %iota_add_fusion, f32[256]{0:T(256)S(1)} %multiply_divide_fusion, s32[256]{0:T(256)S(1)} %all-reduce.1), kind=kOutput, calls=%fused_computation | convolution fusion | flops 1414004736 | bytes 8132608 | tf_op jit(solution)/shard_map/dot_general | solution.py:31
  88.3 37.9 %reduce-scatter.2.cloned.1.call-done = f32[64,3584]{1,0:T(8,128)} async-done(((f32[256,3584]{1,0:T(8,128)}), f32[64,3584]{1,0:T(8,128)}) %reduce-scatter.2.cloned.1.call-update) | async-done | bytes 917520 | tf_op jit(solution)/shard_map/reduce_scatter | solution.py:34
  126.2 49.4 %all-reduce.3 = bf16[64,3584]{1,0:T(8,128)(2,1)} all-reduce(f32[64,3584]{1,0:T(8,128)} %reduce-scatter.2.cloned.1.call-done), channel_id=1, replica_groups=mesh['dp'=4,'vocab'=8] {'vocab'}, use_global_device_ids=true, to_apply=%region_3.4 | all-reduce | flops 229376 | bytes 1376256 | tf_op jit(solution)/shard_map/psum | solution.py:40
  (5 shorter events, 0.0 us)
Async XLA Ops:
  7.2 26.3 %all-gather.2.cloned.1.call-start = ((), (), s32[]{:S(2)}) async-start(), calls=%async_computation.1 | async-start | bytes 2293760 | tf_op jit(solution)/shard_map/all_gather | solution.py:13
  7.9 118.3 %reduce-scatter.2.cloned.1.call-start = ((), (), s32[]{:S(2)}) async-start(), calls=%async_computation.2 | async-start | bytes 4587520 | tf_op jit(solution)/shard_map/reduce_scatter | solution.py:34
  77.7 6.3 %copy-start = (bf16[256,3584]{1,0:T(8,128)(2,1)S(1)}, bf16[256,3584]{1,0:T(8,128)(2,1)}, u32[]{:S(2)}) copy-start(bf16[256,3584]{1,0:T(8,128)(2,1)} %all-gather.2.cloned.1.call-done) | copy-start | bytes 5505028
Sparse Core Ops, SparseCore 0:
  9.5 23.9 all-gather.1
  84.1 42.0 reduce-scatter.1
where the time goes:
time: 183 us; the launch traced here: 182 us
  blocking collectives  102 us (56%)
  waiting for transfers between devices  47.6 us (26%)
  matrix products  15.4 us (8%)
  between operations  14.7 us (8%)
  local copies, waits for them, and re-layouts  2.97 us (2%)
    psum x1, blocking collectives, body(): hidden_grad = lax.psum(group_grad, 'vocab').astype(jnp.bfloat16)  49.4 us
    psum x1, blocking collectives, body(): exp_total = lax.psum(partial_value, ('dp', 'vocab'))  39.3 us
    reduce_scatter x1, waiting for transfers between devices, body(): lax.psum_scatter(jnp.dot(scores_grad, embedding, preferred_element_type=j...  37.9 us
    unnamed x2, blocking collectives  12.8 us
    all_gather x1, waiting for transfers between devices, body(): lax.all_gather(hidden, 'dp', axis=0, tiled=True)  9.04 us
    dot_general x1, matrix products, body(): jnp.dot(scores_grad, embedding, preferred_element_type=jnp.float32)  6.28 us
    dot_general x1, matrix products, body(): lax.dot_general(group_hidden, embedding, (((1,), (1,)), ((), ())), prefer...  4.91 us
    dot_general x1, matrix products, body(): lax.dot_general(scores_grad, group_hidden, (((0,), (0,)), ((), ())), pref...  4.26 us
  transfers between devices with their start and end apart: 2, of which 2 were waited for; matrix products, arithmetic and copies ran while one was open for 4% of the time, Pallas kernels for 0%

commit v1 on v0

--- a/solution.py
+++ b/solution.py
@@ -22,7 +22,7 @@
     partial_value = jnp.sum(exp_terms, axis=1)
     weight = group_weight.astype(jnp.float32)
     device_place = lax.axis_index("dp") * lax.axis_size("vocab") + lax.axis_index("vocab")
-    exp_total = lax.psum(partial_value, ("dp", "vocab"))
+    exp_total = lax.psum(lax.psum(partial_value, "dp"), "vocab")
     factor = weight * (1.0 + 2.0 * z_weight * (soft_cap + jnp.log(exp_total))) / exp_total
     columns = device_place * shard_rows + lax.iota(jnp.int32, shard_rows)
     target_hit = group_targets[:, None] == columns[None, :]

time: 183 us -> 167 us (0.913)
  blocking collectives: 102 us -> 89.6 us
  waiting for transfers between devices: 47.6 us -> 44 us
    psum x1 -> x2, blocking collectives: 39.3 us -> 27.4 us  [body(): exp_total = lax.psum(lax.psum(partial_value, 'dp'), 'vocab')]
    reduce_scatter x1, waiting for transfers between devices: 37.9 us -> 34.3 us  [body(): lax.psum_scatter(jnp.dot(scores_grad, embedding, preferred_element_type=j...]
where the time goes in v1:
time: 167 us
  blocking collectives  89.6 us (54%)
  waiting for transfers between devices  44 us (26%)
  matrix products  15.5 us (9%)
  between operations  14.7 us (9%)
  local copies, waits for them, and re-layouts  2.97 us (2%)
    psum x1, blocking collectives, body(): hidden_grad = lax.psum(group_grad, 'vocab').astype(jnp.bfloat16)  49.4 us
    reduce_scatter x1, waiting for transfers between devices, body(): lax.psum_scatter(jnp.dot(scores_grad, embedding, preferred_element_type=j...  34.3 us
    psum x2, blocking collectives, body(): exp_total = lax.psum(lax.psum(partial_value, 'dp'), 'vocab')  27.4 us
    unnamed x2, blocking collectives  12.8 us
    all_gather x1, waiting for transfers between devices, body(): lax.all_gather(hidden, 'dp', axis=0, tiled=True)  9.04 us
    dot_general x1, matrix products, body(): jnp.dot(scores_grad, embedding, preferred_element_type=jnp.float32)  6.28 us
    dot_general x1, matrix products, body(): lax.dot_general(group_hidden, embedding, (((1,), (1,)), ((), ())), prefer...  4.91 us
    dot_general x1, matrix products, body(): lax.dot_general(scores_grad, group_hidden, (((0,), (0,)), ((), ())), pref...  4.36 us
  transfers between devices with their start and end apart: 2, of which 2 were waited for; matrix products, arithmetic and copies ran while one was open for 4% of the time, Pallas kernels for 0%

profile of v1, /device:TPU:0, one launch (start us, length us, event | category | flops | bytes accessed | tf_op | source)
XLA Modules:
  0.0 167.0 jit_solution(12238479305498964102)
XLA Ops:
  7.2 0.0 all-gather.2.cloned.1.call-start
  7.2 0.7 all-gather.2.cloned.1.call-update
  7.9 0.0 reduce-scatter.2.cloned.1.call-start
  8.0 1.2 dynamic-slice
  9.9 0.9 dynamic-update-slice
  10.7 8.4 %all-reduce = bf16[256]{0:T(256)(128)(2,1)S(1)} all-reduce(bf16[256]{0:T(256)(128)(2,1)S(1)} %dynamic-update-slice), channel_id=1, replica_groups=mesh['dp'=4,'vocab'=8] {'dp'}, use_global_device_ids=true, to_apply=%add | all-reduce | flops 256 | bytes 1024
  19.1 0.9 dynamic-update-slice.1
  20.0 4.5 %all-reduce.1 = s32[256]{0:T(256)S(1)} all-reduce(s32[256]{0:T(256)S(1)} %dynamic-update-slice.1), channel_id=1, replica_groups=mesh['dp'=4,'vocab'=8] {'dp'}, use_global_device_ids=true, to_apply=%add.1 | all-reduce | flops 256 | bytes 2048
  24.4 9.0 %all-gather.2.cloned.1.call-done = bf16[256,3584]{1,0:T(8,128)(2,1)} async-done(((bf16[64,3584]{1,0:T(8,128)(2,1)}), bf16[256,3584]{1,0:T(8,128)(2,1)}) %all-gather.2.cloned.1.call-update) | async-done | bytes 1835024 | tf_op jit(solution)/shard_map/all_gather | solution.py:13
  33.5 4.9 %fusion.1 = (f32[256]{0:T(256)S(1)}, f32[256,768]{1,0:T(8,128)S(1)}) fusion(bf16[256,3584]{1,0:T(8,128)(2,1)} %all-gather.2.cloned.1.call-done, bf16[768,3584]{1,0:T(8,128)(2,1)} %param.5), kind=kOutput, calls=%fused_computation.5 | convolution fusion | flops 1410072320 | bytes 8127488 | tf_op jit(solution)/shard_map/dot_general | solution.py:17
  38.4 5.9 %psum.21 = f32[256]{0:T(256)S(1)} all-reduce(f32[256]{0:T(256)S(1)} %get-tuple-element.2), channel_id=1, replica_groups=mesh['dp'=4,'vocab'=8] {'dp'}, use_global_device_ids=true, to_apply=%region_1.0 | all-reduce | flops 256 | bytes 2048 | tf_op jit(solution)/shard_map/psum | solution.py:25
  44.3 21.5 %psum.22 = f32[256]{0:T(256)S(1)} all-reduce(f32[256]{0:T(256)S(1)} %psum.21), channel_id=1, replica_groups=mesh['dp'=4,'vocab'=8] {'vocab'}, use_global_device_ids=true, to_apply=%region_2.0 | all-reduce | flops 256 | bytes 2048 | tf_op jit(solution)/shard_map/psum | solution.py:25
  65.8 0.0 copy-start
  65.8 6.3 %fusion.2 = f32[256,3584]{1,0:T(8,128)} fusion(bf16[768,3584]{1,0:T(8,128)(2,1)} %param.5, f32[256,768]{1,0:T(8,128)S(1)} %get-tuple-element.3, f32[256]{0:T(256)S(1)} %convert_element_type.12, s32[768]{0:T(1024)S(1)} %iota_add_fusion, f32[256]{0:T(256)S(1)} %multiply_divide_fusion, s32[256]{0:T(256)S(1)} %all-reduce.1), kind=kOutput, calls=%fused_computation.8 | convolution fusion | flops 1411252224 | bytes 9967616 | tf_op jit(solution)/shard_map/dot_general | solution.py:35
  72.1 0.0 reduce-scatter.2.cloned.1.call-update
  72.1 0.0 copy-done
  72.1 4.4 %convolution_convert_fusion = bf16[768,3584]{1,0:T(8,128)(2,1)} fusion(bf16[256,3584]{1,0:T(8,128)(2,1)S(1)} %copy-done, f32[256,768]{1,0:T(8,128)S(1)} %get-tuple-element.3, f32[256]{0:T(256)S(1)} %convert_element_type.12, s32[768]{0:T(1024)S(1)} %iota_add_fusion, f32[256]{0:T(256)S(1)} %multiply_divide_fusion, s32[256]{0:T(256)S(1)} %all-reduce.1), kind=kOutput, calls=%fused_computation | convolution fusion | flops 1414004736 | bytes 8132608 | tf_op jit(solution)/shard_map/dot_general | solution.py:31
  76.4 34.3 %reduce-scatter.2.cloned.1.call-done = f32[64,3584]{1,0:T(8,128)} async-done(((f32[256,3584]{1,0:T(8,128)}), f32[64,3584]{1,0:T(8,128)}) %reduce-scatter.2.cloned.1.call-update) | async-done | bytes 917520 | tf_op jit(solution)/shard_map/reduce_scatter | solution.py:34
  110.7 49.4 %all-reduce.3 = bf16[64,3584]{1,0:T(8,128)(2,1)} all-reduce(f32[64,3584]{1,0:T(8,128)} %reduce-scatter.2.cloned.1.call-done), channel_id=1, replica_groups=mesh['dp'=4,'vocab'=8] {'vocab'}, use_global_device_ids=true, to_apply=%region_4.5 | all-reduce | flops 229376 | bytes 1376256 | tf_op jit(solution)/shard_map/psum | solution.py:40
  (5 shorter events, 0.0 us)
Async XLA Ops:
  7.2 26.3 %all-gather.2.cloned.1.call-start = ((), (), s32[]{:S(2)}) async-start(), calls=%async_computation.1 | async-start | bytes 2293760 | tf_op jit(solution)/shard_map/all_gather | solution.py:13
  7.9 102.8 %reduce-scatter.2.cloned.1.call-start = ((), (), s32[]{:S(2)}) async-start(), calls=%async_computation.2 | async-start | bytes 4587520 | tf_op jit(solution)/shard_map/reduce_scatter | solution.py:34
  65.8 6.3 %copy-start = (bf16[256,3584]{1,0:T(8,128)(2,1)S(1)}, bf16[256,3584]{1,0:T(8,128)(2,1)}, u32[]{:S(2)}) copy-start(bf16[256,3584]{1,0:T(8,128)(2,1)} %all-gather.2.cloned.1.call-done) | copy-start | bytes 5505028
Sparse Core Ops, SparseCore 0:
  9.5 23.9 all-gather.1
  72.2 38.4 reduce-scatter.1

commit v2 on v0

--- a/solution.py
+++ b/solution.py
@@ -37,7 +37,7 @@
         scatter_dimension=0,
         tiled=True,
     )
-    hidden_grad = lax.psum(group_grad, "vocab").astype(jnp.bfloat16)
+    hidden_grad = jnp.sum(lax.all_gather(group_grad, "vocab"), axis=0).astype(jnp.bfloat16)
     return (hidden_grad, table_grad)
 
 

time: 183 us -> 251 us (1.37)
  waiting for transfers between devices: 47.6 us -> 161 us
  blocking collectives: 102 us -> 52.1 us
  other arithmetic: 0.02 us -> 4.41 us
    all_gather x0 -> x1, waiting for transfers between devices: none -> 109 us  [body(): lax.all_gather(group_grad, 'vocab')]
    psum x1 -> x0, blocking collectives: 49.4 us -> none  [body(): hidden_grad = lax.psum(group_grad, 'vocab').astype(jnp.bfloat16)]
    reduce_sum x0 -> x1, other arithmetic: none -> 4.4 us  [body(): jnp.sum(lax.all_gather(group_grad, 'vocab'), axis=0).astype(jnp.bfloat16)]
    reduce_scatter x1, waiting for transfers between devices: 37.9 us -> 42.1 us  [body(): lax.psum_scatter(jnp.dot(scores_grad, embedding, preferred_element_type=j...]
  transfers between devices with their start and end apart: 2 -> 3, of which waited for: 2 -> 3; matrix products, arithmetic and copies ran while one was open for 4% -> 3% of each run, Pallas kernels for 0% -> 0%
where the time goes in v2:
time: 251 us
  waiting for transfers between devices  161 us (64%)
  blocking collectives  52.1 us (21%)
  matrix products  15.4 us (6%)
  between operations  14.4 us (6%)
  other arithmetic  4.41 us (2%)
  local copies, waits for them, and re-layouts  2.97 us (1%)
    all_gather x1, waiting for transfers between devices, body(): lax.all_gather(group_grad, 'vocab')  109 us
    reduce_scatter x1, waiting for transfers between devices, body(): lax.psum_scatter(jnp.dot(scores_grad, embedding, preferred_element_type=j...  42.1 us
    psum x1, blocking collectives, body(): exp_total = lax.psum(partial_value, ('dp', 'vocab'))  39.3 us
    unnamed x2, blocking collectives  12.8 us
    all_gather x1, waiting for transfers between devices, body(): lax.all_gather(hidden, 'dp', axis=0, tiled=True)  9.04 us
    dot_general x1, matrix products, body(): jnp.dot(scores_grad, embedding, preferred_element_type=jnp.float32)  6.23 us
  transfers between devices with their start and end apart: 3, of which 3 were waited for; matrix products, arithmetic and copies ran while one was open for 3% of the time, Pallas kernels for 0%

profile of v2, /device:TPU:0, one launch (start us, length us, event | category | flops | bytes accessed | tf_op | source)
XLA Modules:
  0.0 250.8 jit_solution(16694518400612413729)
XLA Ops:
  7.2 0.0 all-gather.4.cloned.1.call-start
  7.2 0.7 all-gather.4.cloned.1.call-update
  7.9 0.0 reduce-scatter.2.cloned.1.call-start
  8.0 1.2 dynamic-slice
  9.9 0.9 dynamic-update-slice
  10.7 8.4 %all-reduce = bf16[256]{0:T(256)(128)(2,1)S(1)} all-reduce(bf16[256]{0:T(256)(128)(2,1)S(1)} %dynamic-update-slice), channel_id=1, replica_groups=mesh['dp'=4,'vocab'=8] {'dp'}, use_global_device_ids=true, to_apply=%add | all-reduce | flops 256 | bytes 1024
  19.1 0.9 dynamic-update-slice.1
  20.0 4.5 %all-reduce.1 = s32[256]{0:T(256)S(1)} all-reduce(s32[256]{0:T(256)S(1)} %dynamic-update-slice.1), channel_id=1, replica_groups=mesh['dp'=4,'vocab'=8] {'dp'}, use_global_device_ids=true, to_apply=%add.1 | all-reduce | flops 256 | bytes 2048
  24.4 9.0 %all-gather.4.cloned.1.call-done = bf16[256,3584]{1,0:T(8,128)(2,1)} async-done(((bf16[64,3584]{1,0:T(8,128)(2,1)}), bf16[256,3584]{1,0:T(8,128)(2,1)}) %all-gather.4.cloned.1.call-update) | async-done | bytes 1835024 | tf_op jit(solution)/shard_map/all_gather | solution.py:13
  33.5 4.9 %fusion.1 = (f32[256]{0:T(256)S(1)}, f32[256,768]{1,0:T(8,128)S(1)}) fusion(bf16[256,3584]{1,0:T(8,128)(2,1)} %all-gather.4.cloned.1.call-done, bf16[768,3584]{1,0:T(8,128)(2,1)} %param.5), kind=kOutput, calls=%fused_computation.5 | convolution fusion | flops 1410072320 | bytes 8127488 | tf_op jit(solution)/shard_map/dot_general | solution.py:17
  38.4 39.3 %psum.7 = f32[256]{0:T(256)S(1)} all-reduce(f32[256]{0:T(256)S(1)} %get-tuple-element.2), channel_id=1, replica_groups=mesh['dp'=4,'vocab'=8] {'dp','vocab'}, use_global_device_ids=true, to_apply=%region_1.0 | all-reduce | flops 256 | bytes 2048 | tf_op jit(solution)/shard_map/psum | solution.py:25
  77.7 6.2 %fusion.2 = f32[256,3584]{1,0:T(8,128)} fusion(bf16[768,3584]{1,0:T(8,128)(2,1)} %param.5, f32[256,768]{1,0:T(8,128)S(1)} %get-tuple-element.3, f32[256]{0:T(256)S(1)} %convert_element_type.12, s32[768]{0:T(1024)S(1)} %iota_add_fusion, f32[256]{0:T(256)S(1)} %multiply_divide_fusion, s32[256]{0:T(256)S(1)} %all-reduce.1), kind=kOutput, calls=%fused_computation.8 | convolution fusion | flops 1411252224 | bytes 9967616 | tf_op jit(solution)/shard_map/dot_general | solution.py:35
  83.9 0.0 copy-start
  83.9 0.0 reduce-scatter.2.cloned.1.call-update
  84.0 0.0 all-gather.6.cloned.1.call-start
  84.0 42.1 %reduce-scatter.2.cloned.1.call-done = f32[64,3584]{1,0:T(8,128)} async-done(((f32[256,3584]{1,0:T(8,128)}), f32[64,3584]{1,0:T(8,128)}) %reduce-scatter.2.cloned.1.call-update) | async-done | bytes 917520 | tf_op jit(solution)/shard_map/reduce_scatter | solution.py:34
  126.1 0.0 all-gather.6.cloned.1.call-update
  126.1 0.0 copy-done
  126.2 4.3 %convolution_convert_fusion = bf16[768,3584]{1,0:T(8,128)(2,1)} fusion(bf16[256,3584]{1,0:T(8,128)(2,1)S(1)} %copy-done, f32[256,768]{1,0:T(8,128)S(1)} %get-tuple-element.3, f32[256]{0:T(256)S(1)} %convert_element_type.12, s32[768]{0:T(1024)S(1)} %iota_add_fusion, f32[256]{0:T(256)S(1)} %multiply_divide_fusion, s32[256]{0:T(256)S(1)} %all-reduce.1), kind=kOutput, calls=%fused_computation | convolution fusion | flops 1414004736 | bytes 8132608 | tf_op jit(solution)/shard_map/dot_general | solution.py:31
  130.4 109.4 %all-gather.6.cloned.1.call-done = f32[512,3584]{1,0:T(8,128)} async-done(((f32[64,3584]{1,0:T(8,128)}), f32[512,3584]{1,0:T(8,128)}) %all-gather.6.cloned.1.call-update) | async-done | bytes 7340048 | tf_op jit(solution)/shard_map/all_gather | solution.py:40
  239.8 4.4 %reduce_sum.19 = bf16[64,3584]{1,0:T(8,128)(2,1)} reduce(f32[8,64,3584]{2,1,0:T(8,128)} %bitcast.6, f32[]{:T(128)} %constant.9.clone.1), dimensions={0}, to_apply=%region_3.4 | reduce | flops 1605632 | bytes 7798788 | tf_op jit(solution)/shard_map/reduce_sum | solution.py:40
  (5 shorter events, 0.0 us)
Async XLA Ops:
  7.2 26.3 %all-gather.4.cloned.1.call-start = ((), (), s32[]{:S(2)}) async-start(), calls=%async_computation.1 | async-start | bytes 2293760 | tf_op jit(solution)/shard_map/all_gather | solution.py:13
  7.9 118.2 %reduce-scatter.2.cloned.1.call-start = ((), (), s32[]{:S(2)}) async-start(), calls=%async_computation.2 | async-start | bytes 4587520 | tf_op jit(solution)/shard_map/reduce_scatter | solution.py:34
  83.9 42.2 %copy-start = (bf16[256,3584]{1,0:T(8,128)(2,1)S(1)}, bf16[256,3584]{1,0:T(8,128)(2,1)}, u32[]{:S(2)}) copy-start(bf16[256,3584]{1,0:T(8,128)(2,1)} %all-gather.4.cloned.1.call-done) | copy-start | bytes 5505028
  84.0 155.9 %all-gather.6.cloned.1.call-start = ((), (), s32[]{:S(2)}) async-start(), calls=%async_computation.3 | async-start | bytes 8257536 | tf_op jit(solution)/shard_map/all_gather | solution.py:40
Sparse Core Ops, SparseCore 0:
  9.5 23.9 all-gather.3
  84.1 41.9 reduce-scatter.1
  128.3 111.4 all-gather.5
